TPU v7x, 32 devices: a whole 2x2x4 slice. The times are simulated.
32 devices in a mesh: ti: 4 (over z), tj: 8 (over y, x, core).
Axes of the slice: x: 2, y: 2, z: 4, core: 2. Of those that a mesh axis runs over, the one named last changes fastest.
Arguments:
- alignment_source: float32 [32, 128, 64], P('tj', 'ti'), may hold values from -6 to 6
- couple_source: float32 [128, 128, 128], P('ti', 'tj'), may hold values from -6 to 6
- tensor_operand_matrix: float32 [64, 64], replicated, may hold values from -0.75 to 0.75
- tensor_final_matrix: float32 [1024, 128], replicated, may hold values from -0.75 to 0.75
- mixing_content_matrix: float32 [64, 256], replicated, may hold values from -0.75 to 0.75
- mixing_switch_matrix: float32 [64, 256], replicated, may hold values from -0.75 to 0.75
- mixing_score_matrix: float32 [128, 8], replicated, may hold values from -48 to 48, as said below
- mixing_final_matrix: float32 [256, 64], replicated, may hold values from -0.375 to 0.375
- alignment_expand_matrix: float32 [64, 512], replicated, may hold values from -0.75 to 0.75
- alignment_shrink_matrix: float32 [256, 64], replicated, may hold values from -0.375 to 0.375
- couple_expand_matrix: float32 [128, 1024], replicated, may hold values from -0.5 to 0.5
- couple_shrink_matrix: float32 [512, 128], replicated, may hold values from -0.25 to 0.25
Outputs:
- alignment_result: float32 [32, 128, 64], P('tj', 'ti')
- couple_result: float32 [128, 128, 128], P('ti', 'tj')
Inputs may be any that keep to these rules, and one draw needn't show every extreme that they name: `mixing_score_matrix`: each column is one head's logit projection.
All inputs are finite; a program needn't handle non-finite values.
Results may differ from a plain program's by a relative error of at most 0.00026.
Values sent between devices are 32-bit elements; how exact they have to be, the bound alone decides.
A program may use at most 64 MiB of HBM per device.

v0:
```python
import math

import jax
import jax.numpy as jnp
from jax import lax
from jax.sharding import PartitionSpec as P

C_Z = 128
FACTOR_WIDTH = 32
MEAN_GROUPS = 8
GROUP_FEATURES = 32


exact_arithmetic = lax.Precision.HIGHEST
epsilon = 1e-05


def feature_standardize(inputs):
    mean_val = jnp.mean(inputs, axis=-1, keepdims=True)
    centred = inputs - mean_val
    variance = jnp.mean(centred * centred, axis=-1, keepdims=True)
    return centred * lax.rsqrt(variance + epsilon)


def feedforward_block(inputs, gate_up, down):
    hidden = jnp.einsum("...c,cd->...d", inputs, gate_up, precision=exact_arithmetic)
    half_width = down.shape[0]
    activated = jax.nn.silu(hidden[..., :half_width]) * hidden[..., half_width:]
    return jnp.einsum("...c,cd->...d", activated, down, precision=exact_arithmetic)


def shards(
    alignment_source,
    couple_source,
    tensor_operand_matrix,
    tensor_final_matrix,
    mixing_content_matrix,
    mixing_switch_matrix,
    mixing_score_matrix,
    mixing_final_matrix,
    alignment_expand_matrix,
    alignment_shrink_matrix,
    couple_expand_matrix,
    couple_shrink_matrix,
):
    sequence_index = alignment_source.shape[0]
    residue_index = alignment_source.shape[1]
    col_count = couple_source.shape[1]
    tj_count = lax.axis_size("tj")
    sequence_count_all = sequence_index * tj_count
    alignment_standardized = feature_standardize(alignment_source)
    tensor_operands = jnp.einsum(
        "zji,in->zjn", alignment_standardized, tensor_operand_matrix, precision=exact_arithmetic
    )
    left_proj = tensor_operands[..., :FACTOR_WIDTH]
    right_proj = tensor_operands[..., FACTOR_WIDTH:]
    left_all = lax.all_gather(left_proj, "tj", axis=0, tiled=True)
    right_wide = lax.all_gather(right_proj, "ti", axis=1, tiled=True)
    right_all = lax.all_to_all(right_wide, "tj", split_axis=1, concat_axis=0, tiled=True)
    block_size = math.gcd(residue_index, 32)
    block_count = residue_index // block_size
    left_blocks = left_all.reshape(
        sequence_count_all, block_count, block_size, FACTOR_WIDTH
    ).transpose(1, 0, 2, 3)
    pair_blocks = couple_source.reshape(block_count, block_size, col_count, C_Z)

    def pair_block(inputs_pair):
        left_block, pair_rows = inputs_pair
        outer_prod = (
            jnp.einsum("sia,sjb->ijab", left_block, right_all, precision=exact_arithmetic)
            / sequence_count_all
        )
        flattened = outer_prod.reshape(-1, FACTOR_WIDTH * FACTOR_WIDTH)
        update = jnp.dot(
            flattened,
            tensor_final_matrix,
            precision=exact_arithmetic,
            preferred_element_type=jnp.float32,
        )
        pair_mid = pair_rows + update.reshape(pair_rows.shape)
        pair_normed = feature_standardize(pair_mid)
        logits = jnp.einsum(
            "ijc,ch->hij", pair_normed, mixing_score_matrix, precision=exact_arithmetic
        )
        pair_next = pair_mid + feedforward_block(
            pair_normed, couple_expand_matrix, couple_shrink_matrix
        )
        return (pair_next, logits)

    pair_next, logit_blocks = lax.map(pair_block, (left_blocks, pair_blocks))
    couple_result = pair_next.reshape(residue_index, col_count, C_Z)
    local_logits = logit_blocks.transpose(1, 0, 2, 3).reshape(MEAN_GROUPS, residue_index, col_count)
    logits_all = lax.all_gather(local_logits, "tj", axis=2, tiled=True)
    row_max = jnp.max(logits_all, axis=2, keepdims=True)
    exp_terms = jnp.exp(logits_all - row_max)
    weights = exp_terms / jnp.sum(exp_terms, axis=2, keepdims=True)
    sigmoid_switch = jax.nn.sigmoid(
        jnp.einsum(
            "zji,in->zjn", alignment_standardized, mixing_switch_matrix, precision=exact_arithmetic
        )
    )
    sequence_slice = lax.all_gather(alignment_standardized, "ti", axis=1, tiled=True)
    seg_values = jnp.einsum(
        "jzb,bq->jzq", sequence_slice, mixing_content_matrix, precision=exact_arithmetic
    )
    seg_values = seg_values.reshape(
        sequence_index, sequence_slice.shape[1], MEAN_GROUPS, GROUP_FEATURES
    )
    group_mixed = jnp.einsum("hij,sjhc->sihc", weights, seg_values, precision=exact_arithmetic)
    group_mixed = group_mixed.reshape(sequence_index, residue_index, MEAN_GROUPS * GROUP_FEATURES)
    alignment_between = alignment_source + jnp.einsum(
        "xvr,rq->xvq", sigmoid_switch * group_mixed, mixing_final_matrix, precision=exact_arithmetic
    )
    alignment_result = alignment_between + feedforward_block(
        feature_standardize(alignment_between), alignment_expand_matrix, alignment_shrink_matrix
    )
    return (alignment_result, couple_result)


def solution(mesh):
    in_specs = (
        P("tj", "ti", None),
        P("ti", "tj", None),
        P(),
        P(),
        P(),
        P(),
        P(),
        P(),
        P(),
        P(),
        P(),
        P(),
    )
    out_specs = (P("tj", "ti", None), P("ti", "tj", None))
    return jax.shard_map(shards, mesh=mesh, in_specs=in_specs, out_specs=out_specs, check_vma=False)
```

profile of v0, /device:TPU:0, one launch (start us, length us, event | category | flops | bytes accessed | tf_op | source)
XLA Modules:
  0.0 99.3 jit_solution(15225961795344053580)
XLA Ops:
  0.6 0.0 copy-start
  0.6 0.0 copy-start.4
  0.7 1.0 %reduce_sum.65 = f32[4,32]{1,0:T(4,128)S(1)} reduce(f32[4,32,64]{2,1,0:T(8,128)} %param.12, f32[]{:T(128)} %constant.41.clone.1), dimensions={2}, to_apply=%region_0.0 | reduce | flops 8064 | bytes 33284 | tf_op jit(solution)/shard_map/reduce_sum | solution.py:19
  1.7 1.0 %multiply_reduce_fusion.2 = f32[4,32]{1,0:T(4,128)S(1)} fusion(f32[4,32,64]{2,1,0:T(8,128)} %param.12, f32[4,32]{1,0:T(4,128)S(1)} %broadcast_multiply_fusion.2), kind=kLoop, calls=%fused_computation.57 | loop fusion | flops 24448 | bytes 33792 | tf_op jit(solution)/shard_map/reduce_sum | solution.py:21
  2.7 0.9 subtract_multiply_fusion
  3.6 1.0 fusion.45
  4.6 0.1 fusion.52
  4.7 15.7 %all_gather.13 = f32[4,128,32]{2,1,0:T(8,128)S(1)} all-gather(f32[4,32,32]{2,1,0:T(8,128)S(1)} %get-tuple-element.22), channel_id=1, replica_groups=mesh['ti'=4,'tj'=8] {'ti'}, dimensions={1}, use_global_device_ids=true | all-gather | bytes 81920 | tf_op jit(solution)/shard_map/all_gather | solution.py:58
  20.3 0.2 copy.64
  20.5 0.8 reshape.77
  21.3 3.7 %all-to-all-start = ((f32[8,1,2048]{2,1,0:T(1,128)}), f32[8,1,2048]{2,1,0:T(1,128)S(1)}, u32[]{:S(2)}, u32[]{:S(2)}) async-start(f32[8,1,2048]{2,1,0:T(1,128)} %reshape.77), calls=%async_computation | async-start | bytes 131072 | tf_op jit(solution)/shard_map/all_to_all | solution.py:59
  25.1 14.4 %all_gather.12 = f32[4,128,64]{2,1,0:T(8,128)S(1)} all-gather(f32[4,32,64]{2,1,0:T(8,128)S(1)} %subtract_multiply_fusion), channel_id=1, replica_groups=mesh['ti'=4,'tj'=8] {'ti'}, dimensions={1}, use_global_device_ids=true | all-gather | bytes 163840 | tf_op jit(solution)/shard_map/all_gather | solution.py:102
  39.5 0.0 copy-done.4
  39.5 0.6 fusion.39
  40.1 10.1 %all_gather.14 = f32[32,32,32]{2,1,0:T(8,128)S(1)} all-gather(f32[4,32,32]{2,1,0:T(8,128)S(1)} %get-tuple-element.23), channel_id=1, replica_groups=mesh['ti'=4,'tj'=8] {'tj'}, dimensions={0}, use_global_device_ids=true | all-gather | bytes 147456 | tf_op jit(solution)/shard_map/all_gather | solution.py:57
  50.2 0.0 all-to-all-done
  50.2 0.5 broadcast.103
  50.8 0.8 reduce
  51.6 0.2 reshape.78
  51.8 9.1 %multiply_bitcast_fusion = f32[32,16,32,32]{2,3,0,1:T(8,128)} fusion(f32[32,32,32]{2,1,0:T(8,128)S(1)} %all_gather.14, f32[32,16,32,1]{2,1,0,3:T(8,128)S(1)} %bitcast.66), kind=kOutput, calls=%fused_computation | convolution fusion | flops 201850880 | bytes 2293760 | tf_op jit(solution)/shard_map/while/body/eval_jaxpr/sia,sjb->ijab/dot_general | solution.py:70
  60.9 8.9 %copy.41 = f32[32,16,32,32]{3,2,1,0:T(8,128)} copy(f32[32,16,32,32]{2,3,0,1:T(8,128)} %multiply_bitcast_fusion) | data formatting | bytes 4194304 | tf_op jit(solution)/shard_map/while/body/eval_jaxpr/div | solution.py:70
  69.9 6.6 %dot_general.49 = f32[32,16,1024]{2,1,0:T(8,128)S(1)} reshape(f32[32,16,32,32]{3,2,1,0:T(8,128)} %copy.41) | data formatting | bytes 4194304 | tf_op jit(solution)/shard_map/while/body/eval_jaxpr/dot_general | solution.py:74
  76.5 0.0 copy-start.8
  76.5 3.0 %fusion.53 = (f32[32,16]{1,0:T(8,128)S(1)}, f32[32,16,128]{2,1,0:T(8,128)S(1)}) fusion(f32[32,16,128]{2,1,0:T(8,128)} %param.13, f32[32,16,1024]{2,1,0:T(8,128)S(1)} %dot_general.49, f32[1024,128]{1,0:T(8,128)} %param.15), kind=kOutput, calls=%fused_computation.75 | convolution fusion | flops 805436928 | bytes 3147776 | tf_op jit(solution)/shard_map/while/body/eval_jaxpr/dot_general | solution.py:74
  79.5 0.2 multiply_reduce_fusion
  79.8 0.0 copy-done.8
  79.8 2.0 %convolution_bitcast_fusion.1 = f32[8,32,16]{2,0,1:T(8,128)S(1)} fusion(f32[32,16,128]{2,1,0:T(8,128)S(1)} %get-tuple-element.25, f32[32,16]{1,0:T(8,128)S(1)} %add_rsqrt_fusion, f32[32,16]{1,0:T(8,128)S(1)} %broadcast_multiply_fusion, f32[128,8]{0,1:T(8,128)S(1)} %copy-done.8), kind=kOutput, calls=%fused_computation.4 | convolution fusion | flops 6422528 | bytes 286720 | tf_op jit(solution)/shard_map/while/body/eval_jaxpr/ijc,ch->hij/dot_general | solution.py:82
  81.8 0.1 copy.42
  81.9 10.0 %all_gather.15 = f32[8,32,128]{1,0,2:T(8,128)S(1)} all-gather(f32[8,32,16]{1,0,2:T(8,128)S(1)} %copy.42), channel_id=1, replica_groups=mesh['ti'=4,'tj'=8] {'tj'}, dimensions={2}, use_global_device_ids=true | all-gather | bytes 147456 | tf_op jit(solution)/shard_map/all_gather | solution.py:93
  91.9 0.1 reduce_max.9
  92.1 0.1 fusion.18
  92.2 0.0 copy-start.6
  92.2 0.1 divide_bitcast_fusion
  92.3 0.0 copy-start.1
  92.3 0.0 copy-start.3
  92.3 0.7 convolution_bitcast_fusion
  93.0 0.2 copy.45
  93.2 0.2 reshape.63
  93.4 0.0 copy-done.6
  93.4 0.0 copy-start.2
  93.5 0.0 copy-start.7
  93.5 0.3 fusion.3
  93.7 0.0 copy-done.1
  93.7 0.0 copy-done.3
  93.8 0.3 fusion.54
  94.1 0.0 copy-start.5
  94.1 0.2 multiply_reduce_fusion.1
  94.3 0.0 copy-done
  94.3 1.8 %fusion.10 = f32[32,16,1024]{2,1,0:T(8,128)S(1)} fusion(f32[128,1024]{1,0:T(8,128)S(1)} %copy-done, f32[32,16,128]{2,1,0:T(8,128)S(1)} %get-tuple-element.25, f32[32,16]{1,0:T(8,128)S(1)} %add_rsqrt_fusion, f32[32,16]{1,0:T(8,128)S(1)} %broadcast_multiply_fusion), kind=kOutput, calls=%fused_computation.19 | convolution fusion | flops 805437440 | bytes 2887680 | tf_op jit(solution)/shard_map/while/body/eval_jaxpr/...c,cd->...d/dot_general | solution.py:26
  96.1 0.0 copy-done.2
  96.1 0.4 fusion.25
  96.6 0.0 copy-done.7
  96.6 0.9 convolution_add_fusion.2
  97.5 0.0 copy-done.5
  97.5 1.8 %convolution_add_fusion.1 = f32[32,16,128]{2,1,0:T(8,128)} fusion(f32[32,16,128]{2,1,0:T(8,128)S(1)} %get-tuple-element.25, f32[32,16,1024]{2,1,0:T(8,128)S(1)} %fusion.10, f32[512,128]{1,0:T(8,128)S(1)} %copy-done.5), kind=kOutput, calls=%fused_computation.3 | convolution fusion | flops 404029440 | bytes 2883584 | tf_op jit(solution)/shard_map/while/body/eval_jaxpr/...c,cd->...d/dot_general | solution.py:29
  (8 shorter events, 0.1 us)
Async XLA Ops:
  0.6 93.7 %copy-start = (f32[128,1024]{1,0:T(8,128)S(1)}, f32[128,1024]{1,0:T(8,128)}, u32[]{:S(2)}) copy-start(f32[128,1024]{1,0:T(8,128)} %param.22) | copy-start | bytes 1572868
  0.6 38.9 %copy-start.4 = (f32[64,256]{1,0:T(8,128)S(1)}, f32[64,256]{1,0:T(8,128)}, u32[]{:S(2)}) copy-start(f32[64,256]{1,0:T(8,128)} %param.16) | copy-start | bytes 196612
  21.3 28.9 %all-to-all-start = ((f32[8,1,2048]{2,1,0:T(1,128)}), f32[8,1,2048]{2,1,0:T(1,128)S(1)}, u32[]{:S(2)}, u32[]{:S(2)}) async-start(f32[8,1,2048]{2,1,0:T(1,128)} %reshape.77), calls=%async_computation | async-start | bytes 131072 | tf_op jit(solution)/shard_map/all_to_all | solution.py:59
  76.5 3.3 %copy-start.8 = (f32[128,8]{0,1:T(8,128)S(1)}, f32[128,8]{0,1:T(8,128)}, u32[]{:S(2)}) copy-start(f32[128,8]{0,1:T(8,128)} %param.18) | copy-start | bytes 12292
  92.2 1.2 %copy-start.6 = (f32[64,256]{1,0:T(8,128)S(1)}, f32[64,256]{1,0:T(8,128)}, u32[]{:S(2)}) copy-start(f32[64,256]{1,0:T(8,128)} %param.17) | copy-start | bytes 196612
  92.3 1.4 %copy-start.1 = (f32[4,32,64]{2,1,0:T(8,128)S(1)}, f32[4,32,64]{2,1,0:T(8,128)}, u32[]{:S(2)}) copy-start(f32[4,32,64]{2,1,0:T(8,128)} %param.12) | copy-start | bytes 98308
  92.3 1.4 %copy-start.3 = (f32[256,64]{0,1:T(8,128)S(1)}, f32[256,64]{0,1:T(8,128)}, u32[]{:S(2)}) copy-start(f32[256,64]{0,1:T(8,128)} %param.19) | copy-start | bytes 196612
  93.4 2.7 %copy-start.2 = (f32[64,512]{1,0:T(8,128)S(1)}, f32[64,512]{1,0:T(8,128)}, u32[]{:S(2)}) copy-start(f32[64,512]{1,0:T(8,128)} %param.20) | copy-start | bytes 393220
  93.5 3.1 %copy-start.7 = (f32[256,64]{0,1:T(8,128)S(1)}, f32[256,64]{0,1:T(8,128)}, u32[]{:S(2)}) copy-start(f32[256,64]{0,1:T(8,128)} %param.21) | copy-start | bytes 196612
  94.1 3.4 %copy-start.5 = (f32[512,128]{1,0:T(8,128)S(1)}, f32[512,128]{1,0:T(8,128)}, u32[]{:S(2)}) copy-start(f32[512,128]{1,0:T(8,128)} %param.23) | copy-start | bytes 786436
where the time goes:
time: 100 us; the launch traced here: 99.3 us
  blocking collectives  50.2 us (50%)
  matrix products  22 us (22%)
  local copies, waits for them, and re-layouts  18 us (18%)
  other arithmetic  4.55 us (5%)
  starting transfers between devices  3.72 us (4%)
    all_gather x1, blocking collectives, shards(): right_wide = lax.all_gather(right_proj, 'ti', axis=1, tiled=True)  15.7 us
    all_gather x1, blocking collectives, shards(): lax.all_gather(alignment_standardized, 'ti', axis=1, tiled=True)  14.4 us
    all_gather x1, blocking collectives, shards(): left_all = lax.all_gather(left_proj, 'tj', axis=0, tiled=True)  10.1 us
    all_gather x1, blocking collectives, shards(): logits_all = lax.all_gather(local_logits, 'tj', axis=2, tiled=True)  9.99 us
    dot_general x1, matrix products, pair_block(): jnp.einsum('sia,sjb->ijab', left_block, right_all, precision=exact_arithm...  9.11 us
    div x1, local copies, waits for them, and re-layouts, pair_block(): jnp.einsum('sia,sjb->ijab', left_block, right_all, precision=exact_arithm...  8.95 us
    dot_general x1, local copies, waits for them, and re-layouts, pair_block(): jnp.dot(flattened, tensor_final_matrix, precision=exact_arithmetic, prefe...  6.63 us
    all_to_all x1, starting transfers between devices, shards(): lax.all_to_all(right_wide, 'tj', split_axis=1, concat_axis=0, tiled=True)  3.72 us
  transfers between devices with their start and end apart: 1, of which 0 were waited for; matrix products, arithmetic and copies ran while one was open for 1% of the time, Pallas kernels for 0%

commit v1 on v0

v1 whole, which is shorter than its diff:
```python
import functools

import jax
import jax.numpy as jnp
from jax import lax
from jax.experimental import pallas as pl
from jax.experimental.pallas import tpu as pltpu
from jax.sharding import PartitionSpec as P

F32, BF16 = jnp.float32, jnp.bfloat16
HI = lax.Precision.HIGHEST
MESH = pl.DeviceIdType.MESH
LANES = 128
EPS = 1e-05


def ln(x):
    c = x - jnp.mean(x, axis=-1, keepdims=True)
    return c * lax.rsqrt(jnp.mean(c * c, axis=-1, keepdims=True) + EPS)


def split2(x):
    hi = x.astype(BF16)
    return hi, (x - hi.astype(F32)).astype(BF16)


def split3(x):
    hi = x.astype(BF16)
    r = x - hi.astype(F32)
    mid = r.astype(BF16)
    return hi, mid, (r - mid.astype(F32)).astype(BF16)


def bdot(x, w):
    return jnp.dot(x, w, preferred_element_type=F32)


def dot3(x, w):
    xh, xl = split2(x)
    wh, wl = w
    if x.shape[1] % LANES == 0:
        return bdot(
            jnp.concatenate([xh, xl, xh], axis=1), jnp.concatenate([wh, wh, wl], axis=0)
        )
    return bdot(xh, wh) + (bdot(xl, wh) + bdot(xh, wl))


def lane_iota(rows):
    return lax.broadcasted_iota(jnp.int32, (rows, LANES), 1)


def block_transpose(arrs):
    n = len(arrs)
    width = LANES // n
    lane = lane_iota(arrs[0].shape[0])
    arrs = list(arrs)
    bit = n // 2
    while bit:
        step = bit * width
        low = (lane // step) % 2 == 0
        for t in range(n):
            if t & bit == 0:
                x, y = arrs[t], arrs[t + bit]
                arrs[t] = jnp.where(low, x, pltpu.roll(y, step, 1))
                arrs[t + bit] = jnp.where(low, pltpu.roll(x, LANES - step, 1), y)
        bit //= 2
    return arrs


def kernel(nt, nj, dims, *refs):
    rows, toks, cols, ch, cz, width, heads, feat = dims
    hbm = refs[:12]
    out_msa, out_pair = refs[12:14]
    vm = refs[14:26]
    (
        left_own, right_own, norm_own, logit_own,
        left_all, right_all, norm_all, logit_all,
        outer_flat, pair_mid_ref, pair_norm_ref, pair_out, msa_out,
        in_sem, out_sem, left_send, right_send, norm_send, logit_send,
        left_recv, right_recv, norm_recv, logit_recv,
    ) = refs[26:]
    ti, tj = lax.axis_index("ti"), lax.axis_index("tj")
    ratio = toks // cols
    seqs = rows * nj

    order = (0, 2, 1, 3, 4, 5, 6, 7, 8, 9, 10, 11)
    loads = {k: pltpu.make_async_copy(hbm[k], vm[k], in_sem.at[k]) for k in range(12)}
    for k in order:
        loads[k].start()

    barrier = pltpu.get_barrier_semaphore()
    for d in range(1, nj):
        pl.semaphore_signal(barrier, inc=1, device_id=(ti, (tj + d) % nj), device_id_type=MESH)
    for d in range(1, nt):
        pl.semaphore_signal(barrier, inc=1, device_id=((ti + d) % nt, tj), device_id_type=MESH)
    source_ti = tj // ratio
    is_holder = source_ti == ti
    for d in range(nj):
        if d == 0:
            @pl.when(jnp.logical_not(is_holder))
            def _():
                pl.semaphore_signal(
                    barrier, inc=1, device_id=(source_ti, tj), device_id_type=MESH
                )
        else:
            pl.semaphore_signal(
                barrier, inc=1, device_id=(source_ti, (tj + d) % nj), device_id_type=MESH
            )

    loads[0].wait()
    loads[2].wait()
    src = vm[0][...]
    norm = ln(src)
    operand = vm[2][...]
    rep = (
        lax.broadcasted_iota(jnp.int32, (2 * width, LANES), 0)
        == width + lax.broadcasted_iota(jnp.int32, (2 * width, LANES), 1) % width
    ).astype(F32)
    right_w = jnp.dot(operand, rep, precision=HI, preferred_element_type=F32)
    right = jnp.dot(norm, right_w, precision=HI, preferred_element_type=F32)
    groups = LANES // width
    sub8 = lax.broadcasted_iota(jnp.int32, (8, LANES), 0)
    lane8 = lax.broadcasted_iota(jnp.int32, (8, LANES), 1) // width
    for half in range(ratio):
        for s2 in range(0, rows, 2):
            parts = []
            for s in (s2, s2 + 1):
                at = s * toks + half * cols
                acc = jnp.where(
                    lane8 == sub8 // 4, right[at : at + 8],
                    jnp.where(lane8 == 2 + sub8 // 4, right[at + 8 : at + 16], 0.0),
                )
                parts.append(acc + pltpu.roll(acc, 4, 0))
            right_own[half, s2 * 4 : s2 * 4 + 8, :] = jnp.where(sub8 < 4, parts[0], parts[1])
    norm_rep = jnp.concatenate(
        [norm[s * toks : (s + 1) * toks] for s in range(rows) for _ in range(groups)], axis=0
    )
    left = lax.dot_general(
        operand.T[:width], norm_rep, (((1,), (1,)), ((), ())),
        precision=HI, preferred_element_type=F32,
    )
    for s in range(rows):
        acc = left[0:8, s * LANES : (s + 1) * LANES]
        for q in range(1, groups):
            acc = jnp.where(
                lane8 == q, left[q * 8 : q * 8 + 8, s * LANES : (s + 1) * LANES], acc
            )
        left_own[s * 8 : s * 8 + 8, :] = acc
    packed = rows * toks // 2
    norm_own[...] = jnp.concatenate([norm[:packed], norm[packed:]], axis=1)

    greet = (nj - 1) + (nt - 1) + nt * ratio
    @pl.when(is_holder)
    def _():
        pl.semaphore_wait(barrier, greet - 1)

    @pl.when(jnp.logical_not(is_holder))
    def _():
        pl.semaphore_wait(barrier, greet)

    def remote(src_ref, dst_ref, send, recv, device):
        return pltpu.make_async_remote_copy(
            src_ref=src_ref, dst_ref=dst_ref, send_sem=send, recv_sem=recv,
            device_id=device, device_id_type=MESH,
        )

    sends = []
    right_to = []
    for d in range(nt):
        for c in range(ratio):
            k = d * ratio + c
            to = ((ti + d) % nt, ti * ratio + c)
            copy = remote(
                right_own.at[c], right_all.at[tj], right_send.at[k], right_recv.at[tj], to
            )
            if d == 0:
                mine = ti * ratio + c == tj
                right_to.append((copy, mine))

                @pl.when(mine)
                def _():
                    pltpu.make_async_copy(
                        right_own.at[c], right_all.at[tj], right_recv.at[tj]
                    ).start()

                @pl.when(jnp.logical_not(mine))
                def _():
                    copy.start()
            else:
                copy.start()
                sends.append(copy)
    pltpu.make_async_copy(left_own, left_all.at[tj], left_recv.at[tj]).start()
    for d in range(1, nj):
        copy = remote(
            left_own, left_all.at[tj], left_send.at[d], left_recv.at[tj], (ti, (tj + d) % nj)
        )
        copy.start()
        sends.append(copy)
    pltpu.make_async_copy(norm_own, norm_all.at[ti], norm_recv.at[ti]).start()
    for d in range(1, nt):
        copy = remote(
            norm_own, norm_all.at[ti], norm_send.at[d], norm_recv.at[ti], ((ti + d) % nt, tj)
        )
        copy.start()
        sends.append(copy)

    for k in (5, 6, 3, 1):
        loads[k].wait()
    gates_in = dot3(norm, split2(vm[5][...]))
    gates = 1.0 / (1.0 + jnp.exp(-gates_in))
    spread = (
        lax.broadcasted_iota(jnp.int32, (heads, LANES), 0)
        == lax.broadcasted_iota(jnp.int32, (heads, LANES), 1) // (LANES // heads)
    ).astype(F32)
    score = jnp.dot(vm[6][...], spread, precision=HI, preferred_element_type=F32)
    final = vm[3][...]
    final_perm = jnp.concatenate(
        [
            final[(q * 8 + g) * width : (q * 8 + g + 1) * width]
            for g in range(width // groups) for q in range(groups)
        ],
        axis=0,
    )

    for p in range(nj):
        pltpu.make_async_copy(left_own, left_all.at[p], left_recv.at[p]).wait()
        pltpu.make_async_copy(right_own.at[0], right_all.at[p], right_recv.at[p]).wait()

    tiles = cols // 4
    left_2d = left_all.reshape(seqs * 8, LANES)
    right_2d = right_all.reshape(seqs * 4, LANES)
    r_cat = jnp.concatenate(
        [right_2d[pl.ds(t, seqs, stride=4), :] for t in range(tiles)], axis=1
    )
    rh, rm, rl = split3(r_cat)
    r_stack = jnp.concatenate([rh, rm, rh, rm, rl, rh], axis=0)
    for g in range(width // groups):
        lh, lm, ll = split3(left_2d[pl.ds(g, seqs, stride=8), :])
        l_stack = jnp.concatenate([lh, lh, lm, lm, lh, ll], axis=0)
        outer = lax.dot_general(
            l_stack, r_stack, (((0,), (0,)), ((), ())), preferred_element_type=F32
        )
        for t in range(tiles):
            blocks = block_transpose(
                [outer[q * toks : (q + 1) * toks, t * LANES : (t + 1) * LANES] for q in range(groups)]
            )
            for q in range(groups):
                at = (t * groups + q) * toks
                outer_flat[at : at + toks, g * LANES : (g + 1) * LANES] = blocks[q]
    update = jnp.dot(
        outer_flat[...], final_perm, precision=HI, preferred_element_type=F32
    ) * (1.0 / seqs)
    token_of = [q * 4 + t for t in range(tiles) for q in range(groups)]
    pair_in = jnp.concatenate([vm[1][pl.ds(j, toks, stride=cols), :] for j in token_of], axis=0)
    pair_mid = pair_in + update
    pair_mid_ref[...] = pair_mid
    pair_norm = ln(pair_mid)
    pair_norm_ref[...] = pair_norm
    logits = jnp.dot(pair_norm, score, precision=HI, preferred_element_type=F32)
    slot = lane_iota(toks) % cols
    acc = logits[:toks]
    for p in range(1, cols):
        acc = jnp.where(slot == token_of[p], logits[p * toks : (p + 1) * toks], acc)
    logit_own[...] = acc
    pltpu.make_async_copy(logit_own, logit_all.at[tj], logit_recv.at[tj]).start()
    for d in range(1, nj):
        copy = remote(
            logit_own, logit_all.at[tj], logit_send.at[d], logit_recv.at[tj], (ti, (tj + d) % nj)
        )
        copy.start()
        sends.append(copy)

    loads[10].wait()
    loads[11].wait()
    expand = split2(vm[10][...])
    shrink = split2(vm[11][...])
    hid = vm[11].shape[0]
    chunk = cols * toks // 4
    for b in range(4):
        x = pair_norm_ref[b * chunk : (b + 1) * chunk]
        hidden = dot3(x, expand)
        gate = hidden[:, :hid]
        act = gate / (1.0 + jnp.exp(-gate)) * hidden[:, hid:]
        res = pair_mid_ref[b * chunk : (b + 1) * chunk] + dot3(act, shrink)
        for p in range(chunk // toks):
            j = token_of[b * (chunk // toks) + p]
            pair_out[pl.ds(j, toks, stride=cols), :] = res[p * toks : (p + 1) * toks]
    pair_store = pltpu.make_async_copy(pair_out, out_pair, out_sem.at[0])
    pair_store.start()

    loads[4].wait()
    for p in range(nt):
        pltpu.make_async_copy(norm_own, norm_all.at[p], norm_recv.at[p]).wait()
    content = vm[4][...]
    zero = jnp.zeros_like(content)
    content2 = jnp.concatenate(
        [jnp.concatenate([content, zero], axis=1), jnp.concatenate([zero, content], axis=1)], axis=0
    )
    values = dot3(norm_all.reshape(nt * packed, LANES)[...], split2(content2))
    hf = heads * feat
    per = rows // 2
    values = jnp.concatenate(
        [
            jnp.concatenate(
                [
                    values[t * packed + lo * toks : t * packed + (lo + 1) * toks, up * hf : (up + 1) * hf]
                    for t in range(nt)
                ],
                axis=0,
            )
            for up in range(2) for lo in range(per)
        ],
        axis=1,
    )
    values = split2(values)
    for k in (7, 8, 9):
        loads[k].wait()
    mix_final = split2(vm[7][...])
    msa_expand = split2(vm[8][...])
    msa_shrink = split2(vm[9][...])

    for p in range(nj):
        pltpu.make_async_copy(logit_own, logit_all.at[p], logit_recv.at[p]).wait()
    scores = jnp.concatenate(
        [
            jnp.concatenate(block_transpose([logit_all[g + p] for p in range(heads)]), axis=0)
            for g in range(0, nj, heads)
        ],
        axis=1,
    )
    exps = jnp.exp(scores - jnp.max(scores, axis=-1, keepdims=True))
    weights = exps / jnp.sum(exps, axis=-1, keepdims=True)
    mixed = dot3(weights, values)
    head_of = lax.broadcasted_iota(jnp.int32, (toks, hf), 1) // feat
    averaged = []
    for s in range(rows):
        acc = mixed[:toks, s * hf : (s + 1) * hf]
        for h in range(1, heads):
            acc = jnp.where(
                head_of == h, mixed[h * toks : (h + 1) * toks, s * hf : (s + 1) * hf], acc
            )
        averaged.append(acc)
    averaged = jnp.concatenate(averaged, axis=0)
    msa_mid = src + dot3(gates * averaged, mix_final)
    hidden = dot3(ln(msa_mid), msa_expand)
    inner = vm[9].shape[0]
    gate = hidden[:, :inner]
    act = gate / (1.0 + jnp.exp(-gate)) * hidden[:, inner:]
    msa_out[...] = msa_mid + dot3(act, msa_shrink)
    msa_store = pltpu.make_async_copy(msa_out, out_msa, out_sem.at[1])
    msa_store.start()

    for copy in sends:
        copy.wait_send()
    for copy, mine in right_to:
        @pl.when(jnp.logical_not(mine))
        def _():
            copy.wait_send()
    pair_store.wait()
    msa_store.wait()


def shards(nt, nj, *args):
    rows, toks, ch = args[0].shape
    cols, cz = args[1].shape[1:]
    width = args[2].shape[1] // 2
    heads = args[6].shape[1]
    feat = args[4].shape[1] // heads
    dims = (rows, toks, cols, ch, cz, width, heads, feat)
    flat = (args[0].reshape(rows * toks, ch), args[1].reshape(toks * cols, cz)) + args[2:]
    pairs = toks * cols
    packed = rows * toks // 2
    dma = pltpu.SemaphoreType.DMA
    v = lambda *shape: pltpu.VMEM(shape, F32)
    outs = pl.pallas_call(
        functools.partial(kernel, nt, nj, dims),
        out_shape=(
            jax.ShapeDtypeStruct((rows * toks, ch), F32),
            jax.ShapeDtypeStruct((pairs, cz), F32),
        ),
        in_specs=[pl.BlockSpec(memory_space=pl.ANY)] * 12,
        out_specs=(pl.BlockSpec(memory_space=pl.ANY),) * 2,
        scratch_shapes=[v(*a.shape) for a in flat]
        + [
            v(rows * 8, LANES), v(toks // cols, rows * 4, LANES), v(packed, LANES), v(toks, LANES),
            v(nj, rows * 8, LANES), v(nj, rows * 4, LANES), v(nt, packed, LANES), v(nj, toks, LANES),
            v(pairs, width * width), v(pairs, cz), v(pairs, cz), v(pairs, cz), v(rows * toks, ch),
            dma((12,)), dma((2,)), dma((nj,)), dma((nt * toks // cols,)), dma((nt,)), dma((nj,)),
            dma((nj,)), dma((nj,)), dma((nt,)), dma((nj,)),
        ],
        compiler_params=pltpu.CompilerParams(
            collective_id=0, has_side_effects=True, vmem_limit_bytes=48 * 1024 * 1024
        ),
    )(*flat)
    return outs[0].reshape(args[0].shape), outs[1].reshape(args[1].shape)


def solution(mesh):
    in_specs = (P("tj", "ti", None), P("ti", "tj", None)) + (P(),) * 10
    out_specs = (P("tj", "ti", None), P("ti", "tj", None))
    return jax.shard_map(
        functools.partial(shards, mesh.shape["ti"], mesh.shape["tj"]),
        mesh=mesh, in_specs=in_specs, out_specs=out_specs, check_vma=False,
    )
```

time: 100 us -> 32.7 us (0.33)
  blocking collectives: 50.2 us -> 0 us
  matrix products: 22 us -> 0 us
  Pallas kernels: 0 us -> 22 us
  local copies, waits for them, and re-layouts: 18 us -> 9.54 us
  other arithmetic: 4.55 us -> 0 us
  starting transfers between devices: 3.72 us -> 0 us
    all_gather x4 -> x0, blocking collectives: 50.2 us -> none  [the longest x1 15.7 us: shards(): right_wide = lax.all_gather(right_proj, 'ti', axis=1, tiled=True)]
    dot_general x12 -> x0, matrix products: 22 us -> none  [the longest x1 9.11 us: pair_block(): jnp.einsum('sia,sjb->ijab', left_block, right_all, precision=exact_arithm...]
    pallas_call x0 -> x1, Pallas kernels: none -> 22 us  [shards(): pl.pallas_call(functools.partial(kernel, nt, nj, dims), out_shape=(jax.Sh...]
    div x1 -> x0, local copies, waits for them, and re-layouts: 8.95 us -> none  [pair_block(): jnp.einsum('sia,sjb->ijab', left_block, right_all, precision=exact_arithm...]
    unnamed x20 -> x23, local copies, waits for them, and re-layouts: 1.06 us -> 9.54 us
    dot_general x2 -> x0, local copies, waits for them, and re-layouts: 6.74 us -> none  [the longest x1 6.63 us: pair_block(): jnp.dot(flattened, tensor_final_matrix, precision=exact_arithmetic, prefe...]
    all_to_all x1 -> x0, starting transfers between devices: 3.72 us -> none  [shards(): lax.all_to_all(right_wide, 'tj', split_axis=1, concat_axis=0, tiled=True)]
    reduce_sum x5 -> x0, other arithmetic: 2.56 us -> none  [the longest x3 1.4 us: feature_standardize(): variance = jnp.mean(centred * centred, axis=-1, keepdims=True)]
  transfers between devices with their start and end apart: 1 -> 0, of which waited for: 0 -> 0; matrix products, arithmetic and copies ran while one was open for 1% -> 0% of each run, Pallas kernels for 0% -> 0%
where the time goes in v1:
time: 32.7 us; the launch traced here: 32.2 us
  Pallas kernels  22 us (67%)
  local copies, waits for them, and re-layouts  9.54 us (29%)
  between operations  0.71 us (2%)
    pallas_call x1, Pallas kernels, shards(): pl.pallas_call(functools.partial(kernel, nt, nj, dims), out_shape=(jax.Sh...  22 us
    unnamed x23, local copies, waits for them, and re-layouts  9.54 us

profile of v1, /device:TPU:0, one launch (start us, length us, event | category | flops | bytes accessed | tf_op | source)
XLA Modules:
  0.0 32.2 jit_solution(5560026112152412846)
XLA Ops:
  0.6 0.0 copy-start.2
  0.6 0.8 %copy.14.refs_6_ = f32[128,8]{1,0:T(8,128)S(1)} copy(f32[128,8]{0,1:T(8,128)} %param.18) | data formatting | bytes 8192 | tf_op args[6]
  1.5 0.9 %copy.15.refs_7_ = f32[256,64]{1,0:T(8,128)S(1)} copy(f32[256,64]{0,1:T(8,128)} %param.19) | data formatting | bytes 131072 | tf_op args[7]
  2.4 0.0 copy-start.4
  2.4 0.0 copy-start.5
  2.4 1.0 %copy.16.refs_9_ = f32[256,64]{1,0:T(8,128)S(1)} copy(f32[256,64]{0,1:T(8,128)} %param.21) | data formatting | bytes 131072 | tf_op args[9]
  3.4 0.0 copy-done.2
  3.4 0.0 copy-done.4
  3.4 0.0 copy-done.5
  3.4 0.0 copy-start
  3.4 1.0 %copy-done = f32[1024,128]{1,0:T(8,128)S(1)} copy-done((f32[1024,128]{1,0:T(8,128)S(1)}, f32[1024,128]{1,0:T(8,128)}, u32[]{:S(2)}) %copy-start) | copy-done | bytes 524312
  4.5 0.0 copy-start.1
  4.5 1.0 %copy-done.1 = f32[128,1024]{1,0:T(8,128)S(1)} copy-done((f32[128,1024]{1,0:T(8,128)S(1)}, f32[128,1024]{1,0:T(8,128)}, u32[]{:S(2)}) %copy-start.1) | copy-done | bytes 524312
  5.5 0.0 copy-start.3
  5.5 0.9 %copy-done.3 = f32[512,128]{1,0:T(8,128)S(1)} copy-done((f32[512,128]{1,0:T(8,128)S(1)}, f32[512,128]{1,0:T(8,128)}, u32[]{:S(2)}) %copy-start.3) | copy-done | bytes 262168
  6.5 0.0 copy-start.6
  6.5 0.8 %copy-done.6 = f32[64,256]{1,0:T(8,128)S(1)} copy-done((f32[64,256]{1,0:T(8,128)S(1)}, f32[64,256]{1,0:T(8,128)}, u32[]{:S(2)}) %copy-start.6) | copy-done | bytes 65560
  7.3 0.0 copy-start.7
  7.3 0.8 %copy-done.7 = f32[64,256]{1,0:T(8,128)S(1)} copy-done((f32[64,256]{1,0:T(8,128)S(1)}, f32[64,256]{1,0:T(8,128)}, u32[]{:S(2)}) %copy-start.7) | copy-done | bytes 65560
  8.1 0.0 copy-start.8
  8.2 0.8 %copy-done.8 = f32[64,64]{1,0:T(8,128)S(1)} copy-done((f32[64,64]{1,0:T(8,128)S(1)}, f32[64,64]{1,0:T(8,128)}, u32[]{:S(2)}) %copy-start.8) | copy-done | bytes 16408
  8.9 22.0 %shard_map.131 = (f32[128,64]{1,0:T(8,128)S(1)}, f32[512,128]{1,0:T(8,128)S(1)}) custom-call(f32[128,64]{1,0:T(8,128)S(1)} %bitcast.6, f32[512,128]{1,0:T(8,128)S(1)} %bitcast.4, f32[64,64]{1,0:T(8,128)S(1)} %copy-done.8, f32[1024,128]{1,0:T(8,128)S(1)} %copy-done, f32[64,256]{1,0:T(8,128)S(1)} %copy-done.6, f32[64,256]{1,0:T(8,128)S(1)} %copy-done.7, ...), custom_call_target="tpu_custom_call" | custom-call | tf_op jit(solution)/shard_map/pallas_call | solution.py:375
  30.9 0.6 %copy.19 = f32[4,32,64]{2,1,0:T(8,128)} copy(f32[4,32,64]{2,1,0:T(8,128)S(1)} %bitcast.7) | data formatting | bytes 65536
  31.5 0.7 %copy.20 = f32[32,16,128]{2,1,0:T(8,128)} copy(f32[32,16,128]{2,1,0:T(8,128)S(1)} %bitcast.5) | data formatting | bytes 524288
Async XLA Ops:
  0.6 2.8 %copy-start.2 = (f32[32,16,128]{2,1,0:T(8,128)S(1)}, f32[32,16,128]{2,1,0:T(8,128)}, u32[]{:S(2)}) copy-start(f32[32,16,128]{2,1,0:T(8,128)} %param.13) | copy-start | bytes 786436
  2.4 1.0 %copy-start.4 = (f32[64,512]{1,0:T(8,128)S(1)}, f32[64,512]{1,0:T(8,128)}, u32[]{:S(2)}) copy-start(f32[64,512]{1,0:T(8,128)} %refs_8_.1) | copy-start | bytes 393220
  2.4 1.0 %copy-start.5 = (f32[4,32,64]{2,1,0:T(8,128)S(1)}, f32[4,32,64]{2,1,0:T(8,128)}, u32[]{:S(2)}) copy-start(f32[4,32,64]{2,1,0:T(8,128)} %param.12) | copy-start | bytes 98308
  3.4 1.0 %copy-start = (f32[1024,128]{1,0:T(8,128)S(1)}, f32[1024,128]{1,0:T(8,128)}, u32[]{:S(2)}) copy-start(f32[1024,128]{1,0:T(8,128)} %refs_3_.1) | copy-start | bytes 1572868
  4.5 1.0 %copy-start.1 = (f32[128,1024]{1,0:T(8,128)S(1)}, f32[128,1024]{1,0:T(8,128)}, u32[]{:S(2)}) copy-start(f32[128,1024]{1,0:T(8,128)} %refs_10_.1) | copy-start | bytes 1572868
  5.5 0.9 %copy-start.3 = (f32[512,128]{1,0:T(8,128)S(1)}, f32[512,128]{1,0:T(8,128)}, u32[]{:S(2)}) copy-start(f32[512,128]{1,0:T(8,128)} %refs_11_.1) | copy-start | bytes 786436
  6.5 0.8 %copy-start.6 = (f32[64,256]{1,0:T(8,128)S(1)}, f32[64,256]{1,0:T(8,128)}, u32[]{:S(2)}) copy-start(f32[64,256]{1,0:T(8,128)} %refs_4_.1) | copy-start | bytes 196612
  7.3 0.8 %copy-start.7 = (f32[64,256]{1,0:T(8,128)S(1)}, f32[64,256]{1,0:T(8,128)}, u32[]{:S(2)}) copy-start(f32[64,256]{1,0:T(8,128)} %refs_5_.1) | copy-start | bytes 196612
  8.1 0.8 %copy-start.8 = (f32[64,64]{1,0:T(8,128)S(1)}, f32[64,64]{1,0:T(8,128)}, u32[]{:S(2)}) copy-start(f32[64,64]{1,0:T(8,128)} %refs_2_.1) | copy-start | bytes 49156

commit v2 on v1

--- a/solution.py
+++ b/solution.py
@@ -212,7 +212,7 @@
         lax.broadcasted_iota(jnp.int32, (heads, LANES), 0)
         == lax.broadcasted_iota(jnp.int32, (heads, LANES), 1) // (LANES // heads)
     ).astype(F32)
-    score = jnp.dot(vm[6][...], spread, precision=HI, preferred_element_type=F32)
+    score = jnp.dot(vm[6][...].T, spread, precision=HI, preferred_element_type=F32)
     final = vm[3][...]
     final_perm = jnp.concatenate(
         [
@@ -315,9 +315,9 @@
     values = split2(values)
     for k in (7, 8, 9):
         loads[k].wait()
-    mix_final = split2(vm[7][...])
+    mix_final = split2(vm[7][...].T)
     msa_expand = split2(vm[8][...])
-    msa_shrink = split2(vm[9][...])
+    msa_shrink = split2(vm[9][...].T)
 
     for p in range(nj):
         pltpu.make_async_copy(logit_own, logit_all.at[p], logit_recv.at[p]).wait()
@@ -343,7 +343,7 @@
     averaged = jnp.concatenate(averaged, axis=0)
     msa_mid = src + dot3(gates * averaged, mix_final)
     hidden = dot3(ln(msa_mid), msa_expand)
-    inner = vm[9].shape[0]
+    inner = vm[9].shape[1]
     gate = hidden[:, :inner]
     act = gate / (1.0 + jnp.exp(-gate)) * hidden[:, inner:]
     msa_out[...] = msa_mid + dot3(act, msa_shrink)
@@ -367,7 +367,8 @@
     heads = args[6].shape[1]
     feat = args[4].shape[1] // heads
     dims = (rows, toks, cols, ch, cz, width, heads, feat)
-    flat = (args[0].reshape(rows * toks, ch), args[1].reshape(toks * cols, cz)) + args[2:]
+    flat = (args[0].reshape(rows * toks, ch), args[1].reshape(toks * cols, cz)) + args[2:6]
+    flat += (args[6].T, args[7].T, args[8], args[9].T) + args[10:]
     pairs = toks * cols
     packed = rows * toks // 2
     dma = pltpu.SemaphoreType.DMA
@@ -389,7 +390,7 @@
             dma((nj,)), dma((nj,)), dma((nt,)), dma((nj,)),
         ],
         compiler_params=pltpu.CompilerParams(
-            collective_id=0, has_side_effects=True, vmem_limit_bytes=48 * 1024 * 1024
+            collective_id=0, has_side_effects=True
         ),
     )(*flat)
     return outs[0].reshape(args[0].shape), outs[1].reshape(args[1].shape)

time: 32.7 us -> 25.5 us (0.78)
  local copies, waits for them, and re-layouts: 9.54 us -> 3.14 us
  Pallas kernels: 22 us -> 21.5 us
    unnamed x23 -> x2, local copies, waits for them, and re-layouts: 9.54 us -> 3.14 us
    pallas_call x1, Pallas kernels: 22 us -> 21.5 us  [shards(): pl.pallas_call(functools.partial(kernel, nt, nj, dims), out_shape=(jax.Sh...]
where the time goes in v2:
time: 25.5 us; the launch traced here: 25.3 us
  Pallas kernels  21.5 us (84%)
  local copies, waits for them, and re-layouts  3.14 us (12%)
  between operations  0.64 us (3%)
    pallas_call x1, Pallas kernels, shards(): pl.pallas_call(functools.partial(kernel, nt, nj, dims), out_shape=(jax.Sh...  21.5 us
    unnamed x2, local copies, waits for them, and re-layouts  3.14 us

profile of v2, /device:TPU:0, one launch (start us, length us, event | category | flops | bytes accessed | tf_op | source)
XLA Modules:
  0.0 25.3 jit_solution(8633821451258738685)
XLA Ops:
  0.6 21.5 %shard_map.131 = (f32[128,64]{1,0:T(8,128)}, f32[512,128]{1,0:T(8,128)}) custom-call(f32[128,64]{1,0:T(8,128)} %bitcast.9, f32[512,128]{1,0:T(8,128)} %bitcast.8, f32[64,64]{1,0:T(8,128)} %refs_2_.1, f32[1024,128]{1,0:T(8,128)} %refs_3_.1, f32[64,256]{1,0:T(8,128)} %refs_4_.1, f32[64,256]{1,0:T(8,128)} %refs_5_.1, f32[8,128]{1,0:T(8,128)} %bitcast.13, ...), custom_call_target="tpu_custom_call" | custom-call | tf_op jit(solution)/shard_map/pallas_call | solution.py:376
  22.2 1.5 %copy.16 = f32[4,32,64]{2,1,0:T(8,128)} copy(f32[4,32,64]{2,1,0:T(8,128)} %bitcast.12) | data formatting | bytes 65536
  23.6 1.7 %copy.17 = f32[32,16,128]{2,1,0:T(8,128)} copy(f32[32,16,128]{2,1,0:T(8,128)} %bitcast.7) | data formatting | bytes 524288
